TPU v7x, 256 devices: a whole 4x4x8 slice. The times are simulated.
256 devices in a mesh: dp: 64 (over z, x, core), seq: 4 (over y).
Axes of the slice: x: 4, y: 4, z: 8, core: 2. Of those that a mesh axis runs over, the one named last changes fastest.
Arguments:
- tokens: bfloat16 [36864, 3584], P('dp'), may hold values from -6 to 6
- positions: int32 [3, 36864], P(None, 'dp'), may hold values from 0 to 2047
- loss_mask: int32 [36864], P('dp'), may hold values from 0 to 1, as said below
- sample_tokens: int32 [64, 3], replicated, may hold values from 96 to 384, as said below
- dest_slot: int32 [36864], P('dp'), may hold values from 0 to 49151, as said below
- norm_gain: float32 [3584], replicated, may hold values from 0.5 to 1.5
- q_weight: bfloat16 [3584, 2048], P(None, 'seq'), may hold values from -0.09375 to 0.09375
- k_weight: bfloat16 [3584, 512], P(None, 'seq'), may hold values from -0.09375 to 0.09375
- v_weight: bfloat16 [3584, 512], P(None, 'seq'), may hold values from -0.09375 to 0.09375
- q_bias: float32 [2048], P('seq'), may hold values from -3 to 3
- k_bias: float32 [512], P('seq'), may hold values from -3 to 3
- v_bias: float32 [512], P('seq'), may hold values from -3 to 3
- o_weight: bfloat16 [2048, 3584], P('seq'), may hold values from -0.125 to 0.125
Outputs:
- mixed: bfloat16 [49152, 3584], P(('dp', 'seq'))
- token_weight: float32 [49152], P(('dp', 'seq'))
Inputs may be any that keep to these rules, and one draw needn't show every extreme that they name: `sample_tokens`: row r gives the token counts of the samples in the buckets of receiver r, of 384, 192 and 192 slots; each count lies between half of its bucket's slots and all of them. Some receiver has all three buckets full. All counts together equal the number of rows of tokens. `dest_slot`: every row has a slot of its own, and the slots that rows take are exactly the first sample_tokens[r, b] slots of each bucket b of each receiver r. Of the rows of one sender at most 12 go to one receiver; a receiver whose buckets are all full takes exactly 12 rows from every sender. `loss_mask`: the first of each sender's 576 rows is 1.
All inputs are finite; a program needn't handle non-finite values.
Results may differ from a plain program's by a relative error of at most 0.015.
Values may be sent and summed in bfloat16 or wider, within the bound.
A program may use at most 128 MiB of HBM per device.

v0:
```python
import functools
import math

import jax
import jax.numpy as jnp
from jax import lax
from jax.sharding import Mesh
from jax.sharding import PartitionSpec as P

DH = 128
BUCKET = 384
DP = ("dp_0", "dp_1", "dp_2")
DP_SEQ = ("dp_0", "dp_1", "dp_2", "seq")


NORM_EPSILON = 1e-06
ROPE_BASE = 1000000.0


def one_axis_at_a_time(shard, axes):
    return functools.reduce(lax.psum, axes, shard)


def side_by_side(arrays, axis, split_dim, concat_dim, along):
    both = jnp.concatenate(arrays, axis=along)
    whole, at, done = (
        lax.all_to_all(both, axis, split_axis=split_dim, concat_axis=concat_dim, tiled=True),
        0,
        [],
    )
    for a in arrays:
        done.append(lax.slice_in_dim(whole, at, at + a.shape[along], axis=along))
        at += a.shape[along]
    return tuple(done)


def rms_norm(rows_in, gain):
    widened = rows_in.astype(jnp.float32)
    mean_square = jnp.mean(widened * widened, axis=-1, keepdims=True)
    return (widened * lax.rsqrt(mean_square + NORM_EPSILON) * gain).astype(jnp.bfloat16)


def rotary_tables(position_ids, head_size):
    half_size = head_size // 2
    pair_index = jnp.arange(half_size, dtype=jnp.int32)
    inv_freq = jnp.exp(pair_index.astype(jnp.float32) * (-2.0 * math.log(ROPE_BASE) / head_size))
    time_limit = head_size // 8
    height_limit = time_limit + 3 * head_size // 16
    chosen = jnp.where(
        pair_index[None, :] < time_limit,
        position_ids[0][:, None],
        jnp.where(
            pair_index[None, :] < height_limit, position_ids[1][:, None], position_ids[2][:, None]
        ),
    )
    angles = chosen.astype(jnp.float32) * inv_freq[None, :]
    return (jnp.cos(angles), jnp.sin(angles))


def rotate(heads_in, cosine, sine_part):
    half_size = heads_in.shape[-1] // 2
    first_half = heads_in[..., :half_size]
    second_half = heads_in[..., half_size:]
    cosine = cosine[:, None, :]
    sine_part = sine_part[:, None, :]
    return jnp.concatenate(
        [
            first_half * cosine - second_half * sine_part,
            second_half * cosine + first_half * sine_part,
        ],
        axis=-1,
    )


def project(normed, q_weight, k_weight, v_weight, q_bias, k_bias, v_bias):
    queries = (jnp.dot(normed, q_weight, preferred_element_type=jnp.float32) + q_bias).astype(
        jnp.bfloat16
    )
    key_rows = (jnp.dot(normed, k_weight, preferred_element_type=jnp.float32) + k_bias).astype(
        jnp.bfloat16
    )
    value_rows = (jnp.dot(normed, v_weight, preferred_element_type=jnp.float32) + v_bias).astype(
        jnp.bfloat16
    )
    return (queries, key_rows, value_rows)


def rotate_rows(queries, key_rows, position_ids):
    cosine, sine_part = rotary_tables(position_ids, DH)
    row_count = queries.shape[0]
    q_turned = rotate(queries.astype(jnp.float32).reshape(row_count, -1, DH), cosine, sine_part)
    k_turned = rotate(key_rows.astype(jnp.float32).reshape(row_count, -1, DH), cosine, sine_part)
    return (
        q_turned.astype(jnp.bfloat16).reshape(row_count, -1),
        k_turned.astype(jnp.bfloat16).reshape(row_count, -1),
    )


def place_rows(rows_in, target_slots, slot_count):
    flat_rows = rows_in.reshape(slot_count, -1)
    empty = jnp.zeros((slot_count, flat_rows.shape[-1]), flat_rows.dtype)
    return empty.at[target_slots].set(flat_rows, mode="drop")


def attend_group(queries, key_rows, value_rows, lengths):
    block_count = queries.shape[0]
    row_count = queries.shape[1]
    scores = jnp.einsum(
        "bqagd,bkad->bagqk", queries, key_rows, preferred_element_type=jnp.float32
    ) * (1.0 / math.sqrt(DH))
    places = jnp.arange(row_count, dtype=jnp.int32)
    allowed = (places[:, None] >= places[None, :])[None] & (
        places[None, None, :] < lengths[:, None, None]
    )
    scores = jnp.where(allowed[:, None, None], scores, -1e30)
    weights = jax.nn.softmax(scores, axis=-1).astype(jnp.bfloat16)
    context = jnp.einsum(
        "bagqk,bkad->bqagd", weights, value_rows, preferred_element_type=jnp.float32
    )
    live_rows = places[None, :] < lengths[:, None]
    context = jnp.where(live_rows[:, :, None, None, None], context, 0.0).astype(jnp.bfloat16)
    return context.reshape(block_count * row_count, -1)


def attend_buckets(q_rows, k_rows, v_rows, lengths, kv_count, group_size):
    half_bucket = BUCKET // 2
    first_part = attend_group(
        q_rows[:BUCKET].reshape(1, BUCKET, kv_count, group_size, DH),
        k_rows[:BUCKET].reshape(1, BUCKET, kv_count, DH),
        v_rows[:BUCKET].reshape(1, BUCKET, kv_count, DH),
        lengths[:1],
    )
    second_part = attend_group(
        q_rows[BUCKET:].reshape(2, half_bucket, kv_count, group_size, DH),
        k_rows[BUCKET:].reshape(2, half_bucket, kv_count, DH),
        v_rows[BUCKET:].reshape(2, half_bucket, kv_count, DH),
        lengths[1:],
    )
    return jnp.concatenate([first_part, second_part], axis=0)


def per_device(
    tokens,
    positions,
    loss_mask,
    sample_tokens,
    dest_slot,
    norm_gain,
    q_weight,
    k_weight,
    v_weight,
    q_bias,
    k_bias,
    v_bias,
    o_weight,
):
    peer_count = lax.axis_size(DP)
    own_index = lax.axis_index(DP)
    seq_count = lax.axis_size("seq")
    seq_index = lax.axis_index("seq")
    source_rows = tokens.shape[0]
    slot_count = 2 * BUCKET
    capacity = slot_count // peer_count
    head_count = q_weight.shape[1] // DH
    kv_count = k_weight.shape[1] // DH
    group_size = head_count // kv_count
    target_peer = dest_slot // slot_count
    target_local = dest_slot % slot_count
    peer_ids = jnp.arange(peer_count, dtype=jnp.int32)
    one_hot = (target_peer[:, None] == peer_ids[None, :]).astype(jnp.int32)
    ranking = jnp.sum((jnp.cumsum(one_hot, axis=0) - one_hot) * one_hot, axis=1)
    buffer_slot = target_peer * capacity + ranking
    row_ids = jnp.arange(source_rows, dtype=jnp.int32)
    source_of = jnp.zeros((slot_count,), jnp.int32).at[buffer_slot].set(row_ids)
    is_live = jnp.zeros((slot_count,), jnp.int32).at[buffer_slot].set(1) > 0
    info_rows = jnp.concatenate([positions, loss_mask[None, :], target_local[None, :]], axis=0)
    filler = jnp.array([0, 0, 0, 0, slot_count], jnp.int32)[:, None]
    send_info = jnp.where(is_live[None, :], info_rows[:, source_of], filler)
    mask_sum = jnp.sum(loss_mask)
    recv_info = lax.all_to_all(send_info, DP, split_axis=1, concat_axis=1, tiled=True)
    loss_total = one_axis_at_a_time(mask_sum.astype(jnp.float32), DP)
    recv_local = recv_info[4]
    slot_info = (
        jnp.zeros((4, slot_count), jnp.int32).at[:, recv_local].set(recv_info[:4], mode="drop")
    )
    zero_value = jnp.zeros((), jnp.bfloat16)
    q_all, k_all, v_all = project(
        rms_norm(tokens, norm_gain), q_weight, k_weight, v_weight, q_bias, k_bias, v_bias
    )
    q_all, k_all = rotate_rows(q_all, k_all, positions)

    def select_slots(source_array):
        return jnp.where(is_live[:, None], source_array[source_of], zero_value).reshape(
            peer_count, capacity, -1
        )

    q_recv, k_recv, v_recv = side_by_side(
        (select_slots(q_all), select_slots(k_all), select_slots(v_all)), DP, 0, 0, 2
    )
    q_slots = place_rows(q_recv, recv_local, slot_count)
    k_slots = place_rows(k_recv, recv_local, slot_count)
    v_slots = place_rows(v_recv, recv_local, slot_count)
    lengths = sample_tokens[own_index]
    context = attend_buckets(q_slots, k_slots, v_slots, lengths, kv_count, group_size)
    part_rows = slot_count // seq_count
    mixed = lax.psum_scatter(
        jnp.dot(context, o_weight, preferred_element_type=jnp.float32).astype(jnp.bfloat16),
        "seq",
        scatter_dimension=0,
        tiled=True,
    )
    row_scale = peer_count * source_rows / loss_total
    own_mask = lax.dynamic_slice_in_dim(slot_info[3], seq_index * part_rows, part_rows, 0).astype(
        jnp.float32
    )
    return (mixed, own_mask * row_scale)


def solution(mesh):
    finer = Mesh(mesh.devices.reshape(8, 4, 2, mesh.shape["seq"]), ("dp_0", "dp_1", "dp_2", "seq"))
    placed = (
        P(DP, None),
        P(None, DP),
        P(DP),
        P(),
        P(DP),
        P(),
        P(None, "seq"),
        P(None, "seq"),
        P(None, "seq"),
        P("seq"),
        P("seq"),
        P("seq"),
        P("seq", None),
    )
    return jax.shard_map(
        per_device,
        mesh=finer,
        in_specs=placed,
        out_specs=(P(DP_SEQ, None), P(DP_SEQ)),
        check_vma=False,
    )
```

profile of v0, /device:TPU:1, one launch (start us, length us, event | category | flops | bytes accessed | tf_op | source)
XLA Modules:
  0.0 210.6 jit_solution(8668392832558939635)
XLA Ops:
  8.7 1.5 reduce-window.6
  11.4 4.1 %scatter_custom_fusion = s32[768]{0:T(1024)S(1)} fusion(s32[576]{0:T(1024)S(1)} %get-tuple-element.17, s32[576]{0:T(1024)S(1)} %ne.22, s32[]{:T(128)} %constant.35.clone.1), kind=kCustom, calls=%fused_computation.114 | custom fusion | bytes 3076 | tf_op jit(solution)/shard_map/scatter | solution.py:175
  15.5 4.1 %scatter_custom_fusion.1 = s32[768]{0:T(1024)S(1)} fusion(s32[576]{0:T(1024)S(1)} %get-tuple-element.17, s32[576]{0:T(1024)S(1)} %iota.73, s32[]{:T(128)} %constant.35.clone.1), kind=kCustom, calls=%fused_computation.111 | custom fusion | bytes 3076 | tf_op jit(solution)/shard_map/scatter | solution.py:174
  20.7 1.6 gather_fusion
  22.7 0.8 copy.54
  23.5 13.1 %all-to-all-start = ((s32[5,64,12]{2,0,1:T(8,128)}), s32[5,64,12]{2,0,1:T(8,128)S(1)}, u32[]{:S(2)}, u32[]{:S(2)}) async-start(s32[5,64,12]{2,0,1:T(8,128)} %copy.54), calls=%async_computation | async-start | bytes 524288 | tf_op jit(solution)/shard_map/all_to_all | solution.py:180
  36.7 3.2 %fusion = f32[576]{0:T(1024)S(1)} fusion(bf16[576,3584]{1,0:T(8,128)(2,1)} %param.14), kind=kLoop, calls=%fused_computation.12 | loop fusion | flops 6192576 | bytes 4131072 | tf_op jit(solution)/shard_map/reduce_sum | solution.py:39
  40.0 1.3 fusion.15
  41.4 1.9 gather_fusion.3
  43.3 3.6 %fusion.17 = f32[576,1,128]{2,0,1:T(8,128)S(1)} fusion(bf16[3584,128]{1,0:T(8,128)(2,1)S(1)} %copy-done.8, f32[128]{0:T(128)S(1)} %copy-done.12, bf16[576,3584]{1,0:T(8,128)(2,1)} %param.14, f32[3584]{0:T(1024)S(1)} %copy-done.9, f32[576]{0:T(1024)S(1)} %add_rsqrt_fusion), kind=kOutput, calls=%fused_computation.44 | convolution fusion | flops 536961024 | bytes 5358336 | tf_op jit(solution)/shard_map/dot_general | solution.py:79
  46.9 2.0 fusion.29
  48.9 1.6 fusion.34
  50.7 1.9 gather_fusion.2
  52.6 6.7 %fusion.7 = f32[576,512]{1,0:T(8,128)} fusion(bf16[3584,512]{1,0:T(8,128)(2,1)} %param.20, f32[512]{0:T(512)S(1)} %copy-done.10, bf16[576,3584]{1,0:T(8,128)(2,1)} %param.14, f32[3584]{0:T(1024)S(1)} %copy-done.9, f32[576]{0:T(1024)S(1)} %add_rsqrt_fusion), kind=kOutput, calls=%fused_computation.28 | convolution fusion | flops 2123071488 | bytes 8997120 | tf_op jit(solution)/shard_map/dot_general | solution.py:76
  59.3 1.7 reshape.701
  60.9 0.9 subtract_convert_fusion
  62.7 2.9 %gather_fusion.1 = bf16[768,512]{1,0:T(8,128)(2,1)S(1)} fusion(bf16[576,512]{1,0:T(8,128)(2,1)S(1)} %bitcast.109, s32[1024]{0:T(1024)S(1)} %pad_clamp_fusion), kind=kCustom, calls=%fused_computation.1 | custom fusion | bytes 1575936 | tf_op jit(solution)/shard_map/gather | solution.py:193
  66.2 1.4 pad_maximum_fusion
  67.6 10.4 %all-to-all-start.1 = ((bf16[64,12,768]{2,1,0:T(8,128)(2,1)}), bf16[64,12,768]{2,1,0:T(8,128)(2,1)S(1)}, u32[]{:S(2)}, u32[]{:S(2)}) async-start(bf16[64,12,768]{2,1,0:T(8,128)(2,1)} %pad_maximum_fusion), calls=%async_computation.1 | async-start | bytes 3145728 | tf_op jit(solution)/shard_map/all_to_all | solution.py:27
  81.4 35.7 %all-to-all-done.1 = bf16[64,12,768]{2,1,0:T(8,128)(2,1)S(1)} async-done(((bf16[64,12,768]{2,1,0:T(8,128)(2,1)}), bf16[64,12,768]{2,1,0:T(8,128)(2,1)S(1)}, u32[]{:S(2)}, u32[]{:S(2)}) %all-to-all-start.1) | async-done | bytes 1179680 | tf_op jit(solution)/shard_map/all_to_all | solution.py:27
  117.2 1.1 reshape.772
  118.4 6.5 %scatter_custom_fusion.4 = bf16[768,512]{1,0:T(8,128)(2,1)S(1)} fusion(s32[768]{0:T(1024)S(1)} %fusion.42, bf16[768,512]{1,0:T(8,128)(2,1)} %reshape.772, bf16[]{:T(256)} %constant.37.clone.1), kind=kCustom, calls=%fused_computation.56 | custom fusion | bytes 786944 | tf_op jit(solution)/shard_map/scatter | solution.py:102
  124.9 4.3 %scatter_custom_fusion.3 = bf16[768,128]{1,0:T(8,128)(2,1)S(1)} fusion(s32[768]{0:T(1024)S(1)} %fusion.42, bf16[768,128]{1,0:T(8,128)(2,1)S(1)} %reshape.764, bf16[]{:T(256)} %constant.37.clone.1), kind=kCustom, calls=%fused_computation.89 | custom fusion | bytes 196610 | tf_op jit(solution)/shard_map/scatter | solution.py:102
  129.6 4.5 %scatter_custom_fusion.2 = bf16[768,128]{1,0:T(8,128)(2,1)S(1)} fusion(s32[768]{0:T(1024)S(1)} %fusion.42, bf16[768,128]{1,0:T(8,128)(2,1)S(1)} %reshape.756, bf16[]{:T(256)} %constant.37.clone.1), kind=kCustom, calls=%fused_computation.91 | custom fusion | bytes 196610 | tf_op jit(solution)/shard_map/scatter | solution.py:102
  134.2 1.3 fusion.55
  137.8 0.9 fusion.9
  138.9 7.4 %convolution_convert_fusion = bf16[768,3584]{1,0:T(8,128)(2,1)} fusion(bf16[512,3584]{1,0:T(8,128)(2,1)} %param.26, bf16[384,512]{1,0:T(8,128)(2,1)S(1)} %bitcast.115, bf16[384,512]{1,0:T(8,128)(2,1)S(1)} %copy.62), kind=kOutput, calls=%fused_computation.15 | convolution fusion | flops 2822897664 | bytes 9961472 | tf_op jit(solution)/shard_map/dot_general | solution.py:207
  148.3 13.7 %psum.21 = f32[]{:T(128)} all-reduce(f32[]{:T(128)S(6)} %convert_element_type.103), channel_id=1, replica_groups=mesh['dp_0'=8,'dp_1'=4,'dp_2'=2,'seq'=4] {'dp_0'}, use_global_device_ids=true, to_apply=%region_16.17 | all-reduce | flops 1 | bytes 8 | tf_op jit(solution)/shard_map/psum | solution.py:21
  162.0 8.9 %psum.22 = f32[]{:T(128)} all-reduce(f32[]{:T(128)} %psum.21), channel_id=1, replica_groups=mesh['dp_0'=8,'dp_1'=4,'dp_2'=2,'seq'=4] {'dp_1'}, use_global_device_ids=true, to_apply=%region_17.18 | all-reduce | flops 1 | bytes 8 | tf_op jit(solution)/shard_map/psum | solution.py:21
  170.9 7.9 %psum.23 = f32[]{:T(128)} all-reduce(f32[]{:T(128)} %psum.22), channel_id=1, replica_groups=mesh['dp_0'=8,'dp_1'=4,'dp_2'=2,'seq'=4] {'dp_2'}, use_global_device_ids=true, to_apply=%region_18.19 | all-reduce | flops 1 | bytes 8 | tf_op jit(solution)/shard_map/psum | solution.py:21
  179.9 4.3 %scatter_custom_fusion.5 = s32[4,768]{0,1:T(8,128)S(1)} fusion(s32[768]{0:T(1024)S(1)} %fusion.42, s32[768,4]{1,0:T(8,128)S(1)} %copy.64, s32[]{:T(128)} %constant.35.clone.1), kind=kCustom, calls=%fused_computation.68 | custom fusion | bytes 12292 | tf_op jit(solution)/shard_map/scatter | solution.py:184
  185.0 18.8 %reduce-scatter.2.cloned.1.call-done = bf16[192,3584]{1,0:T(8,128)(2,1)} async-done(((bf16[768,3584]{1,0:T(8,128)(2,1)}), bf16[192,3584]{1,0:T(8,128)(2,1)}) %reduce-scatter.2.cloned.1.call-update) | async-done | bytes 1376272 | tf_op jit(solution)/shard_map/reduce_scatter | solution.py:206
  (97 shorter events, 14.8 us)
Async XLA Ops:
  7.2 32.8 %copy-start = (bf16[3584,128]{1,0:T(8,128)(2,1)S(1)}, bf16[3584,128]{1,0:T(8,128)(2,1)}, u32[]{:S(2)}) copy-start(bf16[3584,128]{1,0:T(8,128)(2,1)} %param.22) | copy-start | bytes 2752516
  7.2 15.4 %copy-start.7 = (s32[5]{0:T(128)S(1)}, s32[5]{0:T(128)}, u32[]{:S(2)}) copy-start(s32[5]{0:T(128)} %constant.93.clone) | copy-start | bytes 64
  7.2 29.5 %copy-start.4 = (s32[3,576]{1,0:T(4,128)S(1)}, s32[3,576]{1,0:T(4,128)}, u32[]{:S(2)}) copy-start(s32[3,576]{1,0:T(4,128)} %param.15) | copy-start | bytes 20740
  23.5 16.4 %copy-start.9 = (f32[3584]{0:T(1024)S(1)}, f32[3584]{0:T(1024)}, u32[]{:S(2)}) copy-start(f32[3584]{0:T(1024)} %param.19) | copy-start | bytes 43012
  23.5 16.4 %copy-start.11 = (f32[128]{0:T(128)S(1)}, f32[128]{0:T(128)}, u32[]{:S(2)}) copy-start(f32[128]{0:T(128)} %param.25) | copy-start | bytes 1540
  23.5 44.1 %all-to-all-start = ((s32[5,64,12]{2,0,1:T(8,128)}), s32[5,64,12]{2,0,1:T(8,128)S(1)}, u32[]{:S(2)}, u32[]{:S(2)}) async-start(s32[5,64,12]{2,0,1:T(8,128)} %copy.54), calls=%async_computation | async-start | bytes 524288 | tf_op jit(solution)/shard_map/all_to_all | solution.py:180
  36.6 3.4 %copy-start.1 = (bf16[576,3584]{1,0:T(8,128)(2,1)S(1)}, bf16[576,3584]{1,0:T(8,128)(2,1)}, u32[]{:S(2)}) copy-start(bf16[576,3584]{1,0:T(8,128)(2,1)} %param.14) | copy-start | bytes 12386308
  40.0 3.3 %copy-start.8 = (bf16[3584,128]{1,0:T(8,128)(2,1)S(1)}, bf16[3584,128]{1,0:T(8,128)(2,1)}, u32[]{:S(2)}) copy-start(bf16[3584,128]{1,0:T(8,128)(2,1)} %param.21) | copy-start | bytes 2752516
  40.0 3.3 %copy-start.12 = (f32[128]{0:T(128)S(1)}, f32[128]{0:T(128)}, u32[]{:S(2)}) copy-start(f32[128]{0:T(128)} %param.24) | copy-start | bytes 1540
  46.9 5.7 %copy-start.10 = (f32[512]{0:T(512)S(1)}, f32[512]{0:T(512)}, u32[]{:S(2)}) copy-start(f32[512]{0:T(512)} %param.23) | copy-start | bytes 6148
  67.6 10.5 %copy-start.6 = (s32[64,3]{0,1:T(4,128)S(1)}, s32[64,3]{0,1:T(4,128)}, u32[]{:S(2)}) copy-start(s32[64,3]{0,1:T(4,128)} %param.17) | copy-start | bytes 2308
  67.6 13.7 %copy-start.3 = (s32[5,64,12]{2,0,1:T(8,128)}, s32[5,64,12]{2,0,1:T(8,128)S(1)}, u32[]{:S(2)}) copy-start(s32[5,64,12]{2,0,1:T(8,128)S(1)} %all-to-all-done) | copy-start | bytes 46084
  67.6 49.5 %all-to-all-start.1 = ((bf16[64,12,768]{2,1,0:T(8,128)(2,1)}), bf16[64,12,768]{2,1,0:T(8,128)(2,1)S(1)}, u32[]{:S(2)}, u32[]{:S(2)}) async-start(bf16[64,12,768]{2,1,0:T(8,128)(2,1)} %pad_maximum_fusion), calls=%async_computation.1 | async-start | bytes 3145728 | tf_op jit(solution)/shard_map/all_to_all | solution.py:27
  78.0 125.7 %reduce-scatter.2.cloned.1.call-start = ((), (), s32[]{:S(2)}) async-start(), calls=%async_computation.3 | async-start | bytes 6881280 | tf_op jit(solution)/shard_map/reduce_scatter | solution.py:206
  135.8 0.9 copy-start.2
  146.3 0.7 copy-start.5
  146.3 33.2 %slice-start = ((s32[5,64,12]{2,0,1:T(8,128)}), s32[4,64,12]{2,0,1:T(4,128)S(1)}, s32[]{:S(2)}) async-start(s32[5,64,12]{2,0,1:T(8,128)} %copy-done.3), calls=%async_computation.4 | async-start | bytes 262144 | tf_op jit(solution)/shard_map/slice | solution.py:184
Sparse Core Ops, SparseCore 0:
  146.4 57.2 reduce-scatter.1
where the time goes:
time: 211 us
  waiting for transfers between devices  54.5 us (26%)
  local copies, waits for them, and re-layouts  45 us (21%)
  blocking collectives  30.6 us (15%)
  starting transfers between devices  23.6 us (11%)
  matrix products  22.2 us (11%)
  other arithmetic  18.8 us (9%)
  between operations  16 us (8%)
    all_to_all x1, waiting for transfers between devices, side_by_side(): lax.all_to_all(both, axis, split_axis=split_dim, concat_axis=concat_dim,...  35.7 us
    psum x3, blocking collectives, one_axis_at_a_time(): return functools.reduce(lax.psum, axes, shard)  30.6 us
    reduce_scatter x1, waiting for transfers between devices, per_device(): lax.psum_scatter(jnp.dot(context, o_weight, preferred_element_type=jnp.fl...  18.8 us
    scatter x3, local copies, waits for them, and re-layouts, place_rows(): return empty.at[target_slots].set(flat_rows, mode='drop')  15.3 us
    all_to_all x1, starting transfers between devices, per_device(): lax.all_to_all(send_info, DP, split_axis=1, concat_axis=1, tiled=True)  13.1 us
    all_to_all x1, starting transfers between devices, side_by_side(): lax.all_to_all(both, axis, split_axis=split_dim, concat_axis=concat_dim,...  10.4 us
    dot_general x1, matrix products, per_device(): jnp.dot(context, o_weight, preferred_element_type=jnp.float32)  7.37 us
    gather x6, local copies, waits for them, and re-layouts, select_slots(): source_array[source_of]  6.93 us
  transfers between devices with their start and end apart: 3, of which 2 were waited for; matrix products, arithmetic and copies ran while one was open for 19% of the time, Pallas kernels for 0%

commit v1 on v0

v1 whole, which is shorter than its diff:
```python
import functools
import math

import jax
import jax.numpy as jnp
from jax import lax
from jax.experimental import pallas as pl
from jax.experimental.pallas import tpu as pltpu
from jax.sharding import Mesh
from jax.sharding import PartitionSpec as P

DH = 128
BUCKET = 384
DP = ("dp_0", "dp_1", "dp_2")
DP_SEQ = ("dp_0", "dp_1", "dp_2", "seq")
PEERS = 64
SLOTS = 2 * BUCKET
WIDE = 768
HALF = 384
META = 384

NORM_EPSILON = 1e-06
ROPE_BASE = 1000000.0
MESH = pl.DeviceIdType.MESH


def rms_norm(rows_in, gain):
    widened = rows_in.astype(jnp.float32)
    mean_square = jnp.mean(widened * widened, axis=-1, keepdims=True)
    return (widened * lax.rsqrt(mean_square + NORM_EPSILON) * gain).astype(jnp.bfloat16)


def rotary_tables(position_ids, head_size):
    half_size = head_size // 2
    pair_index = jnp.arange(half_size, dtype=jnp.int32)
    inv_freq = jnp.exp(pair_index.astype(jnp.float32) * (-2.0 * math.log(ROPE_BASE) / head_size))
    time_limit = head_size // 8
    height_limit = time_limit + 3 * head_size // 16
    chosen = jnp.where(
        pair_index[None, :] < time_limit,
        position_ids[0][:, None],
        jnp.where(
            pair_index[None, :] < height_limit, position_ids[1][:, None], position_ids[2][:, None]
        ),
    )
    angles = chosen.astype(jnp.float32) * inv_freq[None, :]
    return (jnp.cos(angles), jnp.sin(angles))


def rotate(heads_in, cosine, sine_part):
    half_size = heads_in.shape[-1] // 2
    first_half = heads_in[..., :half_size]
    second_half = heads_in[..., half_size:]
    cosine = cosine[:, None, :]
    sine_part = sine_part[:, None, :]
    return jnp.concatenate(
        [
            first_half * cosine - second_half * sine_part,
            second_half * cosine + first_half * sine_part,
        ],
        axis=-1,
    )


def attend_group(queries, key_rows, value_rows, lengths):
    block_count = queries.shape[0]
    row_count = queries.shape[1]
    scores = jnp.einsum(
        "bqagd,bkad->bagqk", queries, key_rows, preferred_element_type=jnp.float32
    ) * (1.0 / math.sqrt(DH))
    places = jnp.arange(row_count, dtype=jnp.int32)
    allowed = (places[:, None] >= places[None, :])[None] & (
        places[None, None, :] < lengths[:, None, None]
    )
    scores = jnp.where(allowed[:, None, None], scores, -1e30)
    weights = jax.nn.softmax(scores, axis=-1).astype(jnp.bfloat16)
    context = jnp.einsum(
        "bagqk,bkad->bqagd", weights, value_rows, preferred_element_type=jnp.float32
    )
    live_rows = places[None, :] < lengths[:, None]
    context = jnp.where(live_rows[:, :, None, None, None], context, 0.0).astype(jnp.bfloat16)
    return context.reshape(block_count * row_count, -1)


def attend_buckets(q_rows, k_rows, v_rows, lengths, kv_count, group_size):
    half_bucket = BUCKET // 2
    first_part = attend_group(
        q_rows[:BUCKET].reshape(1, BUCKET, kv_count, group_size, DH),
        k_rows[:BUCKET].reshape(1, BUCKET, kv_count, DH),
        v_rows[:BUCKET].reshape(1, BUCKET, kv_count, DH),
        lengths[:1],
    )
    second_part = attend_group(
        q_rows[BUCKET:].reshape(2, half_bucket, kv_count, group_size, DH),
        k_rows[BUCKET:].reshape(2, half_bucket, kv_count, DH),
        v_rows[BUCKET:].reshape(2, half_bucket, kv_count, DH),
        lengths[1:],
    )
    return jnp.concatenate([first_part, second_part], axis=0)


def peer_coords(index):
    return {"dp_0": index // 8, "dp_1": lax.rem(index // 2, 4), "dp_2": lax.rem(index, 2)}


def exchange_kernel(main_in, tail_in, meta_in, main_out, tail_out, meta_out, send_sems, recv_sems, own_sems):
    me = (lax.axis_index("dp_0") * 4 + lax.axis_index("dp_1")) * 2 + lax.axis_index("dp_2")
    pairs = ((meta_in, meta_out), (main_in, main_out), (tail_in, tail_out))
    barrier = pltpu.get_barrier_semaphore()

    @pl.loop(1, PEERS)
    def _(step):
        peer = lax.rem(me + step, PEERS)
        pl.semaphore_signal(barrier, inc=1, device_id=peer_coords(peer), device_id_type=MESH)

    own = [
        pltpu.make_async_copy(src.at[me], dst.at[me], own_sems.at[i])
        for i, (src, dst) in enumerate(pairs)
    ]
    for copy in own:
        copy.start()
    pl.semaphore_wait(barrier, PEERS - 1)

    @pl.loop(1, PEERS)
    def _(step):
        peer = lax.rem(me + step, PEERS)
        for i, (src, dst) in enumerate(pairs):
            pltpu.make_async_remote_copy(
                src_ref=src.at[peer],
                dst_ref=dst.at[me],
                send_sem=send_sems.at[i],
                recv_sem=recv_sems.at[i],
                device_id=peer_coords(peer),
                device_id_type=MESH,
            ).start()

    for copy in own:
        copy.wait()
    for i, (src, dst) in enumerate(pairs):
        whole = dst.at[pl.ds(0, PEERS - 1)]
        pltpu.make_async_copy(whole, whole, recv_sems.at[i]).wait()
        whole = src.at[pl.ds(0, PEERS - 1)]
        pltpu.make_async_copy(whole, whole, send_sems.at[i]).wait()


def exchange(main, tail, meta):
    shapes = [jax.ShapeDtypeStruct(a.shape, a.dtype) for a in (main, tail, meta)]
    return pl.pallas_call(
        exchange_kernel,
        out_shape=shapes,
        in_specs=[pl.BlockSpec(memory_space=pl.ANY)] * 3,
        out_specs=[pl.BlockSpec(memory_space=pl.ANY)] * 3,
        scratch_shapes=[
            pltpu.SemaphoreType.DMA((3,)),
            pltpu.SemaphoreType.DMA((3,)),
            pltpu.SemaphoreType.DMA((3,)),
        ],
        compiler_params=pltpu.CompilerParams(collective_id=0, has_side_effects=True),
    )(main, tail, meta)


def per_device(
    tokens,
    positions,
    loss_mask,
    sample_tokens,
    dest_slot,
    norm_gain,
    q_weight,
    k_weight,
    v_weight,
    q_bias,
    k_bias,
    v_bias,
    o_weight,
):
    own_index = lax.axis_index(DP)
    seq_count = lax.axis_size("seq")
    seq_index = lax.axis_index("seq")
    source_rows = tokens.shape[0]
    head_count = q_weight.shape[1] // DH
    kv_count = k_weight.shape[1] // DH
    group_size = head_count // kv_count
    bf16, f32 = jnp.bfloat16, jnp.float32

    peer = dest_slot // SLOTS
    value = (dest_slot % SLOTS) * 2 + loss_mask + 1
    rows = jnp.arange(source_rows, dtype=jnp.int32)
    same = (peer[:, None] == peer[None, :]) & (rows[:, None] > rows[None, :])
    rank = jnp.sum(same.astype(jnp.int32), axis=1)

    out_row = jnp.arange(PEERS * 8, dtype=jnp.int32)
    out_peer, out_lane = out_row // 8, out_row % 8
    hit = out_peer[:, None] == peer[None, :]
    pick_main = (hit & (out_lane[:, None] == rank[None, :])).astype(bf16)
    pick_tail = (hit & ((out_lane % 4)[:, None] + 8 == rank[None, :])).astype(bf16)
    meta_rank = jnp.arange(256, dtype=jnp.int32)
    meta_rank = jnp.where(meta_rank < 128, meta_rank % 8, 8 + meta_rank % 4)
    to_peer = (jnp.arange(PEERS, dtype=jnp.int32)[:, None] == peer[None, :]).astype(f32)
    spread = jnp.where(rank[:, None] == meta_rank[None, :], value[:, None], 0).astype(f32)
    meta = jnp.dot(to_peer, spread, precision=lax.Precision.HIGHEST).astype(jnp.int32)
    mask_sum = jnp.broadcast_to(jnp.sum(loss_mask), (PEERS, 128))
    meta = jnp.concatenate([meta, mask_sum], axis=1).reshape(PEERS, 1, META)

    normed = rms_norm(tokens, norm_gain)
    weight = jnp.concatenate([q_weight, k_weight, v_weight], axis=1)
    bias = jnp.concatenate([q_bias, k_bias, v_bias])
    qkv = (jnp.dot(normed, weight, preferred_element_type=f32) + bias).astype(bf16)
    cosine, sine = rotary_tables(positions, DH)
    turned = rotate(qkv[:, :640].astype(f32).reshape(source_rows, 5, DH), cosine, sine)
    qkv = jnp.concatenate([turned.astype(bf16).reshape(source_rows, 640), qkv[:, 640:]], axis=1)

    main = jnp.dot(pick_main, qkv, preferred_element_type=f32).astype(bf16)
    tail = jnp.dot(pick_tail, qkv, preferred_element_type=f32).astype(bf16)
    tail = jnp.where((out_lane < 4)[:, None], tail[:, :HALF], tail[:, HALF:])
    main, tail, meta = exchange(
        main.reshape(PEERS, 8, WIDE), tail.reshape(PEERS, 8, HALF), meta
    )
    main, tail = main.reshape(PEERS * 8, WIDE), tail.reshape(PEERS * 8, HALF)
    main_value = meta[:, 0, :8].reshape(-1)
    tail_value = meta[:, 0, 128:136].reshape(-1)
    loss_total = jnp.sum(meta[:, 0, 256]).astype(f32)

    slot = jnp.arange(SLOTS, dtype=jnp.int32)[:, None]
    put_main = slot * 2 + 1 == main_value - (main_value - 1) % 2
    put_main = put_main & (main_value > 0)
    put_tail = (slot * 2 + 1 == tail_value - (tail_value - 1) % 2) & (tail_value > 0)
    put_low = put_tail & (out_lane < 4)
    put_high = put_tail & (out_lane >= 4)
    placed = jnp.dot(put_main.astype(bf16), main, preferred_element_type=f32) + jnp.concatenate(
        [
            jnp.dot(put_low.astype(bf16), tail, preferred_element_type=f32),
            jnp.dot(put_high.astype(bf16), tail, preferred_element_type=f32),
        ],
        axis=1,
    )
    placed = placed.astype(bf16)
    flags = jnp.sum(jnp.where(put_main, (main_value - 1) % 2, 0), axis=1) + jnp.sum(
        jnp.where(put_low, (tail_value - 1) % 2, 0), axis=1
    )

    lengths = sample_tokens[own_index]
    context = attend_buckets(
        placed[:, :512], placed[:, 512:640], placed[:, 640:], lengths, kv_count, group_size
    )
    part_rows = SLOTS // seq_count
    mixed = lax.psum_scatter(
        jnp.dot(context, o_weight, preferred_element_type=jnp.float32).astype(jnp.bfloat16),
        "seq",
        scatter_dimension=0,
        tiled=True,
    )
    row_scale = PEERS * source_rows / loss_total
    own_mask = lax.dynamic_slice_in_dim(flags, seq_index * part_rows, part_rows, 0).astype(f32)
    return (mixed, own_mask * row_scale)


def solution(mesh):
    finer = Mesh(mesh.devices.reshape(8, 4, 2, mesh.shape["seq"]), ("dp_0", "dp_1", "dp_2", "seq"))
    placed = (
        P(DP, None),
        P(None, DP),
        P(DP),
        P(),
        P(DP),
        P(),
        P(None, "seq"),
        P(None, "seq"),
        P(None, "seq"),
        P("seq"),
        P("seq"),
        P("seq"),
        P("seq", None),
    )
    return jax.shard_map(
        per_device,
        mesh=finer,
        in_specs=placed,
        out_specs=(P(DP_SEQ, None), P(DP_SEQ)),
        check_vma=False,
    )
```

time: 211 us -> 152 us (0.72)
  Pallas kernels: 0 us -> 40.7 us
  local copies, waits for them, and re-layouts: 45 us -> 5.96 us
  blocking collectives: 30.6 us -> 0 us
  starting transfers between devices: 23.6 us -> 0.04 us
  other arithmetic: 18.8 us -> 10.9 us
  waiting for transfers between devices: 54.5 us -> 56.8 us
    pallas_call x0 -> x1, Pallas kernels: none -> 40.7 us  [exchange(): pl.pallas_call(exchange_kernel, out_shape=shapes, in_specs=[pl.BlockSpec(...]
    reduce_scatter x1, waiting for transfers between devices: 18.8 us -> 56.8 us  [per_device(): lax.psum_scatter(jnp.dot(context, o_weight, preferred_element_type=jnp.fl...]
    all_to_all x2 -> x0, waiting for transfers between devices: 35.7 us -> none  [the longest x1 35.7 us: side_by_side(): lax.all_to_all(both, axis, split_axis=split_dim, concat_axis=concat_dim,...]
    psum x3 -> x0, blocking collectives: 30.6 us -> none  [one_axis_at_a_time(): return functools.reduce(lax.psum, axes, shard)]
    scatter x6 -> x0, local copies, waits for them, and re-layouts: 27.7 us -> none  [the longest x3 15.3 us: place_rows(): return empty.at[target_slots].set(flat_rows, mode='drop')]
    all_to_all x2 -> x0, starting transfers between devices: 23.5 us -> none  [the longest x1 13.1 us: per_device(): lax.all_to_all(send_info, DP, split_axis=1, concat_axis=1, tiled=True)]
    gather x9 -> x0, local copies, waits for them, and re-layouts: 8.83 us -> none  [the longest x6 6.93 us: select_slots(): source_array[source_of]]
    reduce_sum x2 -> x4, other arithmetic: 0.67 us -> 3.17 us  [the longest x1 1.46 us: per_device(): loss_total = jnp.sum(meta[:, 0, 256]).astype(f32)]
  transfers between devices with their start and end apart: 3 -> 1, of which waited for: 2 -> 1; matrix products, arithmetic and copies ran while one was open for 19% -> 2% of each run, Pallas kernels for 0% -> 0%
where the time goes in v1:
time: 152 us
  waiting for transfers between devices  56.8 us (37%)
  Pallas kernels  40.7 us (27%)
  matrix products  22.2 us (15%)
  between operations  15.1 us (10%)
  other arithmetic  10.9 us (7%)
  local copies, waits for them, and re-layouts  5.96 us (4%)
    reduce_scatter x1, waiting for transfers between devices, per_device(): lax.psum_scatter(jnp.dot(context, o_weight, preferred_element_type=jnp.fl...  56.8 us
    pallas_call x1, Pallas kernels, exchange(): pl.pallas_call(exchange_kernel, out_shape=shapes, in_specs=[pl.BlockSpec(...  40.7 us
    dot_general x1, matrix products, per_device(): jnp.dot(context, o_weight, preferred_element_type=jnp.float32)  7.38 us
    dot_general x1, matrix products, per_device(): jnp.dot(normed, weight, preferred_element_type=f32) + bias  6.01 us
    reduce_sum x1, other arithmetic, rms_norm(): mean_square = jnp.mean(widened * widened, axis=-1, keepdims=True)  3.21 us
  transfers between devices with their start and end apart: 1, of which 1 were waited for; matrix products, arithmetic and copies ran while one was open for 2% of the time, Pallas kernels for 0%

profile of v1, /device:TPU:1, one launch (start us, length us, event | category | flops | bytes accessed | tf_op | source)
XLA Modules:
  0.0 151.7 jit_solution(6610770596508091634)
XLA Ops:
  7.3 0.6 copy-done
  7.9 0.5 slice.71
  8.7 3.2 %fusion = f32[576]{0:T(1024)S(1)} fusion(bf16[576,3584]{1,0:T(8,128)(2,1)} %param.13), kind=kLoop, calls=%fused_computation.2 | loop fusion | flops 6192576 | bytes 4131072 | tf_op jit(solution)/shard_map/reduce_sum | solution.py:29
  12.1 6.0 %add_convert_fusion = bf16[576,768]{1,0:T(8,128)(2,1)S(1)} fusion(bf16[3584,128]{1,0:T(8,128)(2,1)} %param.21, bf16[3584,128]{1,0:T(8,128)(2,1)} %param.20, bf16[3584,512]{1,0:T(8,128)(2,1)} %param.19, bf16[576,3584]{1,0:T(8,128)(2,1)S(1)} %copy-done.1, f32[3584]{0:T(1024)S(1)} %copy-done.10, f32[576]{0:T(1024)S(1)} %add_rsqrt_fusion, ...), kind=kOutput, calls=%fused_computation.21 | convolution fusion | flops 3196551168 | bytes 10538240 | tf_op jit(solution)/shard_map/dot_general | solution.py:208
  18.3 0.5 copy-done.3
  18.8 0.6 fusion.104
  19.4 0.3 convert_reduce_fusion
  19.8 0.5 convolution_convert_fusion.3
  20.2 0.7 concatenate.26
  20.9 0.7 reshape.543.meta_in
  21.8 0.5 copy.33
  22.3 0.7 fusion.75
  23.3 0.9 convolution_convert_fusion.1
  24.2 1.8 %fusion.26.main_in = bf16[64,8,768]{2,1,0:T(8,128)(2,1)} fusion(s32[576]{0:T(1024)S(1)} %convert_reduce_fusion, s32[576]{0:T(1024)S(1)} %get-tuple-element.25, s32[512]{0:T(512)S(1)} %get-tuple-element.36, s32[512]{0:T(512)S(1)} %get-tuple-element.37, bf16[576,128]{0,1:T(8,128)(2,1)S(1)} %copy.34, bf16[576,640]{0,1:T(8,128)(2,1)S(1)} %bitcast.94), kind=kOutput, calls=%fused_computation.44 | convolution fusion | flops 456032256 | bytes 1679872 | tf_op jit(solution)/shard_map/dot_general | solution.py:213
  26.0 0.9 fusion.66.tail_in
  26.8 40.7 %shard_map.140 = (bf16[64,8,768]{2,1,0:T(8,128)(2,1)}, bf16[64,8,384]{2,1,0:T(8,128)(2,1)}, s32[64,1,384]{2,1,0:T(1,128)}) custom-call(bf16[64,8,768]{2,1,0:T(8,128)(2,1)} %fusion.26.main_in, bf16[64,8,384]{2,1,0:T(8,128)(2,1)} %fusion.66.tail_in, s32[64,1,384]{2,1,0:T(1,128)} %reshape.543.meta_in), custom_call_target="tpu_custom_call" | custom-call | tf_op jit(solution)/shard_map/pallas_call | solution.py:148
  67.5 1.0 slice_reduce_fusion.2
  68.8 1.7 %fusion.29 = f32[768,384]{1,0:T(8,128)S(1)} fusion(s32[512]{0:T(512)S(1)} %get-tuple-element.29, s32[768]{0:T(1024)S(1)} %multiply_add_fusion, pred[512]{0:T(512)(128)(4,1)S(1)} %broadcast_compare_fusion.1, pred[512]{0:T(512)(128)(4,1)S(1)} %broadcast_compare_fusion.2, bf16[64,8,384]{2,1,0:T(8,128)(2,1)} %get-tuple-element.7), kind=kOutput, calls=%fused_computation.47 | convolution fusion | flops 303169536 | bytes 1579008 | tf_op jit(solution)/shard_map/dot_general | solution.py:232
  70.5 0.6 fusion.15
  71.1 0.9 fusion.12
  72.1 0.6 iota_compare_fusion.7
  73.2 0.5 fusion.105
  73.9 0.6 fusion.33
  74.5 0.3 copy.42
  74.9 0.6 fusion.14
  75.4 0.5 fusion.13
  76.0 0.9 fusion.28
  77.0 7.4 %convolution_convert_fusion = bf16[768,3584]{1,0:T(8,128)(2,1)} fusion(bf16[512,3584]{1,0:T(8,128)(2,1)} %param.25, bf16[384,512]{1,0:T(8,128)(2,1)S(1)} %bitcast.96, bf16[384,512]{1,0:T(8,128)(2,1)S(1)} %copy.43), kind=kOutput, calls=%fused_computation.5 | convolution fusion | flops 2822897664 | bytes 9961472 | tf_op jit(solution)/shard_map/dot_general | solution.py:248
  84.5 1.5 slice_reduce_fusion
  86.6 0.8 select_reduce_fusion
  87.4 0.6 convert_multiply_fusion.3
  88.1 56.8 %reduce-scatter.2.cloned.1.call-done = bf16[192,3584]{1,0:T(8,128)(2,1)} async-done(((bf16[768,3584]{1,0:T(8,128)(2,1)}), bf16[192,3584]{1,0:T(8,128)(2,1)}) %reduce-scatter.2.cloned.1.call-update) | async-done | bytes 1376272 | tf_op jit(solution)/shard_map/reduce_scatter | solution.py:247
  (57 shorter events, 2.4 us)
Async XLA Ops:
  7.2 0.7 copy-start
  7.2 137.7 %reduce-scatter.2.cloned.1.call-start = ((), (), s32[]{:S(2)}) async-start(), calls=%async_computation.1 | async-start | bytes 6881280 | tf_op jit(solution)/shard_map/reduce_scatter | solution.py:247
  8.6 3.3 %copy-start.5 = (f32[512]{0:T(512)S(1)}, f32[512]{0:T(512)}, u32[]{:S(2)}) copy-start(f32[512]{0:T(512)} %param.22) | copy-start | bytes 6148
  8.6 3.3 %copy-start.6 = (f32[128]{0:T(128)S(1)}, f32[128]{0:T(128)}, u32[]{:S(2)}) copy-start(f32[128]{0:T(128)} %param.24) | copy-start | bytes 1540
  8.6 3.3 %copy-start.7 = (f32[128]{0:T(128)S(1)}, f32[128]{0:T(128)}, u32[]{:S(2)}) copy-start(f32[128]{0:T(128)} %param.23) | copy-start | bytes 1540
  8.7 3.4 %copy-start.1 = (bf16[576,3584]{1,0:T(8,128)(2,1)S(1)}, bf16[576,3584]{1,0:T(8,128)(2,1)}, u32[]{:S(2)}) copy-start(bf16[576,3584]{1,0:T(8,128)(2,1)} %param.13) | copy-start | bytes 12386308
  8.7 3.4 %copy-start.10 = (f32[3584]{0:T(1024)S(1)}, f32[3584]{0:T(1024)}, u32[]{:S(2)}) copy-start(f32[3584]{0:T(1024)} %param.18) | copy-start | bytes 43012
  18.1 0.7 copy-start.3
  18.1 0.7 copy-start.4
  18.1 1.6 %copy-start.2 = (s32[3,576]{1,0:T(4,128)S(1)}, s32[3,576]{1,0:T(4,128)}, u32[]{:S(2)}) copy-start(s32[3,576]{1,0:T(4,128)} %param.14) | copy-start | bytes 20740
  67.5 3.0 %copy-start.9 = (bf16[64,8,384]{2,1,0:T(8,128)(2,1)S(1)}, bf16[64,8,384]{2,1,0:T(8,128)(2,1)}, u32[]{:S(2)}) copy-start(bf16[64,8,384]{2,1,0:T(8,128)(2,1)} %get-tuple-element.7) | copy-start | bytes 1179652
  68.8 2.3 %copy-start.8 = (bf16[64,8,768]{2,1,0:T(8,128)(2,1)S(1)}, bf16[64,8,768]{2,1,0:T(8,128)(2,1)}, u32[]{:S(2)}) copy-start(bf16[64,8,768]{2,1,0:T(8,128)(2,1)} %get-tuple-element.6) | copy-start | bytes 2359300
Sparse Core Ops, SparseCore 0:
  84.6 60.2 reduce-scatter.1
